TPU v7x, 256 devices: a whole 4x4x8 slice. The times are simulated.
256 devices in a mesh: seq: 16 (over z, core), vocab: 16 (over y, x).
Axes of the slice: x: 4, y: 4, z: 8, core: 2. Of those that a mesh axis runs over, the one named last changes fastest.
Arguments:
- probe_states: bfloat16 [3, 16384, 6144], P(None, 'seq', 'vocab'), may hold values from -6 to 6
- final_states: bfloat16 [16384, 6144], P('seq', 'vocab'), may hold values from -6 to 6
- translator: bfloat16 [3, 6144, 6144], P(None, 'vocab', 'seq'), may hold values from -0.078125 to 0.078125
- translator_bias: float32 [3, 6144], P(None, 'seq'), may hold values from -4 to 4
- norm_gain: float32 [6144], P('seq'), may hold values from 0.5 to 1.5
- unembed: bfloat16 [32768, 6144], P('vocab', 'seq'), may hold values from -0.21875 to 0.21875
- answer_rows: int32 [16, 32], P('seq'), may hold values from 0 to 1023, as said below
- answer_count: int32 [16], P('seq'), may hold values from 1 to 32, 256 in all
- targets: int32 [16, 32], P('seq'), may hold values from 0 to 32767
Outputs:
- answer_logprob: float32 [4, 16, 32], P(None, 'seq')
- answer_kl: float32 [3, 16, 32], P(None, 'seq')
Inputs may be any that keep to these rules, and one draw needn't show every extreme that they name: `answer_rows`: each row holds 32 different positions. `answer_count`: the counts sum to 256, and some sequence has 32.
All inputs are finite; a program needn't handle non-finite values. No bound on the sum of `answer_count` on one device may be relied on, other than what follows from the above.
Results may differ from a plain program's by a relative error of at most 0.00099.
Values may be sent and summed in bfloat16 or wider, within the bound.
No kernel may reach another device: no remote copies, remote signals or barrier semaphores. Data moves between devices by JAX's collectives and lax.ppermute only.
A program may use at most 64 MiB of HBM per device.

v0:
```python
import math
import jax
import jax.numpy as jnp
from jax import lax
from jax.sharding import Mesh
from jax.sharding import PartitionSpec as P

D = 6144
LAYERS = 3
FLAG_DEV = 16
CAP = 32
SEQ = ("seq_0", "seq_1")
VOCAB = ("vocab_0", "vocab_1")


def gathered_by_axis(value, axes, dim):
    for axis in reversed(axes):
        value = lax.all_gather(value, axis, axis=dim, tiled=True)
    return value


def sent_together(arrays, axis, dim, along):
    widths = [math.prod(a.shape[along:]) for a in arrays]
    both = jnp.concatenate(
        [a.reshape(*a.shape[:along], w) for a, w in zip(arrays, widths)], axis=along
    )
    out = lax.all_gather(both, axis, axis=dim, tiled=True)
    blocks = jnp.split(out, [sum(widths[:k]) for k in range(1, len(widths))], axis=along)
    return tuple((b.reshape(*out.shape[:along], *a.shape[along:]) for a, b in zip(arrays, blocks)))


def split_up(value, dim, count):
    before, after = (value.shape[:dim], value.shape[dim + 1 :])
    return jnp.moveaxis(value.reshape(*before, count, -1, *after), dim, 0)


def summed_on_arrival(value, axis, dim):
    blocks = split_up(value, dim, lax.axis_size(axis))
    arrived = lax.all_to_all(blocks, axis, split_axis=0, concat_axis=0, tiled=True)
    return arrived.sum(axis=0)


def over_axes(value, axes):
    for axis in axes:
        value = lax.psum(value, axis)
    return value


def body(
    probe_states,
    final_states,
    translator,
    translator_bias,
    norm_gain,
    unembed,
    answer_rows,
    answer_count,
    targets,
):
    seq_count = lax.axis_size(SEQ)
    seq_index = lax.axis_index(SEQ)
    vocab_index = lax.axis_index(VOCAB)
    width_in = probe_states.shape[2]
    width_out = translator.shape[2]
    vocab_part = unembed.shape[0]
    picks = answer_rows[0]
    local = jnp.concatenate(
        [jnp.take(probe_states, picks, axis=1), jnp.take(final_states, picks, axis=0)[None]], axis=0
    )
    gathered = gathered_by_axis(local, SEQ, 1)
    offset = seq_count // 2 * FLAG_DEV
    counts_all, targets_all = sent_together((answer_count, targets), SEQ, 0, 1)
    starts = jnp.cumsum(counts_all) - counts_all
    ends = starts + counts_all
    packed_index = jnp.arange(seq_count * FLAG_DEV, dtype=jnp.int32)
    source = jnp.sum((ends[None, :] <= packed_index[:, None]).astype(jnp.int32), axis=1)
    matches = source[:, None] == jnp.arange(seq_count, dtype=jnp.int32)[None, :]
    slot = packed_index - jnp.sum(jnp.where(matches, starts[None, :], 0), axis=1)
    flat = jnp.roll(source * CAP + slot, offset)
    rows = jnp.take(gathered, flat, axis=1)
    own_rows = FLAG_DEV
    flat_targets = jnp.take(targets_all.reshape(-1), flat)
    row_targets = lax.dynamic_slice_in_dim(flat_targets, seq_index * own_rows, own_rows)
    total_rows = rows.shape[1]
    in_pos = vocab_index * width_in + jnp.arange(width_in, dtype=jnp.int32)
    out_pos = seq_index * width_out + jnp.arange(width_out, dtype=jnp.int32)
    identity = (in_pos[:, None] == out_pos[None, :]).astype(jnp.bfloat16)
    carried = jnp.einsum("lrd,de->rle", rows, identity, preferred_element_type=jnp.float32)
    mapped = jnp.einsum(
        "lrd,lde->rle", rows[:LAYERS], translator, preferred_element_type=jnp.float32
    )
    partial_value = carried + jnp.concatenate([mapped, jnp.zeros_like(carried[:, :1])], axis=1)
    summed = lax.psum(partial_value, VOCAB)
    bias_rows = jnp.concatenate([translator_bias, jnp.zeros((1, width_out), jnp.float32)], axis=0)
    lensed = summed + bias_rows[None, :, :]
    squares = jnp.sum(lensed * lensed, axis=2)
    own_square = summed_on_arrival(squares, SEQ, 0)
    scaled = (lensed * norm_gain[None, None, :]).astype(jnp.bfloat16)
    product = jnp.einsum("rld,vd->rlv", scaled, unembed, preferred_element_type=jnp.float32)
    term = lax.psum_scatter(
        product.reshape(own_rows * lax.axis_size(SEQ), (LAYERS + 1) * vocab_part),
        SEQ,
        scatter_dimension=0,
        tiled=True,
    )
    factor = lax.rsqrt(own_square / D + 1e-05)
    logits = term.reshape(own_rows, LAYERS + 1, vocab_part) * factor[:, :, None]
    expz = jnp.exp(logits)
    total_exp = jnp.sum(expz, axis=2)
    final_logits = logits[:, LAYERS:]
    cross = jnp.sum(expz[:, LAYERS:] * (final_logits - logits[:, :LAYERS]), axis=2)
    local_ids = row_targets - vocab_index * vocab_part
    target_hit = jnp.arange(vocab_part, dtype=jnp.int32)[None, :] == local_ids[:, None]
    picked = jnp.sum(jnp.where(target_hit[:, None, :], logits, 0.0), axis=2)
    total_exp, cross, picked = (
        over_axes(total_exp, VOCAB),
        over_axes(cross, VOCAB),
        over_axes(picked, VOCAB),
    )
    log_total = jnp.log(total_exp)
    logprob = picked - log_total
    divergence = cross / total_exp[:, LAYERS:] - log_total[:, LAYERS:] + log_total[:, :LAYERS]
    slots = jnp.arange(CAP, dtype=jnp.int32)
    live = slots < answer_count[0]
    results = jnp.concatenate([logprob, divergence], axis=1)
    every_result = lax.all_gather(results, SEQ, axis=0, tiled=True)
    my_start = jnp.sum(jnp.where(jnp.arange(seq_count, dtype=jnp.int32) == seq_index, starts, 0))
    wanted = (jnp.minimum(my_start + slots, total_rows - 1) + offset) % total_rows
    mine = jnp.take(every_result, wanted, axis=0)
    logprob = mine[:, : LAYERS + 1]
    divergence = mine[:, LAYERS + 1 :]
    out_logprob = jnp.where(live[:, None], logprob, 0.0).T[:, None, :]
    out_divergence = jnp.where(live[:, None], divergence, 0.0).T[:, None, :]
    return (out_logprob, out_divergence)


def solution(mesh):
    split = Mesh(mesh.devices.reshape(8, 2, 4, 4), ("seq_0", "seq_1", "vocab_0", "vocab_1"))
    return jax.shard_map(
        body,
        mesh=split,
        in_specs=(
            P(None, SEQ, VOCAB),
            P(SEQ, VOCAB),
            P(None, VOCAB, SEQ),
            P(None, SEQ),
            P(SEQ),
            P(VOCAB, SEQ),
            P(SEQ, None),
            P(SEQ),
            P(SEQ, None),
        ),
        out_specs=(P(None, SEQ, None), P(None, SEQ, None)),
        check_vma=False,
    )
```

profile of v0, /device:TPU:1, one launch (start us, length us, event | category | flops | bytes accessed | tf_op | source)
XLA Modules:
  0.0 305.5 jit_solution(11106795249357113970)
XLA Ops:
  7.2 0.8 compare_and_fusion
  8.7 1.9 gather_fusion.2
  10.6 0.8 gather_fusion.1
  11.6 4.9 %all_gather.13 = bf16[4,64,384]{2,1,0:T(8,128)(2,1)} all-gather(bf16[4,32,384]{2,1,0:T(8,128)(2,1)S(1)} %pad_maximum_fusion), channel_id=1, replica_groups=mesh['seq_0'=8,'seq_1'=2,'vocab_0'=4,'vocab_1'=4] {'seq_1'}, dimensions={1}, use_global_device_ids=true | all-gather | bytes 294912 | tf_op jit(solution)/shard_map/all_gather | solution.py:18
  17.3 18.5 %all-gather = s32[16,1,33]{2,1,0:T(1,128)S(1)} all-gather(s32[1,1,33]{2,1,0:T(1,128)S(1)} %add_bitcast_fusion), channel_id=1, replica_groups=mesh['seq_0'=8,'seq_1'=2,'vocab_0'=4,'vocab_1'=4] {'seq_0','seq_1'}, dimensions={0}, use_global_device_ids=true | all-gather | bytes 2244 | tf_op jit(solution)/shard_map/all_gather | solution.py:27
  37.1 1.9 gather_fusion
  39.1 13.6 %all-gather.4.cloned.1.call-done = bf16[4,512,384]{2,1,0:T(8,128)(2,1)} async-done(((bf16[4,64,384]{2,1,0:T(8,128)(2,1)}), bf16[4,512,384]{2,1,0:T(8,128)(2,1)}) %all-gather.4.cloned.1.call-update) | async-done | bytes 1572880 | tf_op jit(solution)/shard_map/all_gather | solution.py:18
  52.7 3.8 %copy.39 = bf16[4,512,384]{2,0,1:T(4,128)(2,1)} copy(bf16[4,512,384]{2,1,0:T(8,128)(2,1)} %all-gather.4.cloned.1.call-done) | data formatting | bytes 3145728 | tf_op jit(solution)/shard_map/all_gather | solution.py:18
  56.5 2.9 gather_fusion.3
  59.4 1.9 convolution_bitcast_fusion
  61.2 1.8 bitcast_add_fusion
  63.8 100.1 %all-reduce.6.cloned.1.call-done = f32[256,4,384]{0,2,1:T(8,128)} async-done(((f32[256,4,384]{0,2,1:T(8,128)}), f32[256,4,384]{0,2,1:T(8,128)}) %all-reduce.6.cloned.1.call-update) | async-done | bytes 1572880 | tf_op jit(solution)/shard_map/psum | solution.py:93
  163.9 7.6 %fusion.2 = f32[256,4,2048]{0,2,1:T(8,128)} fusion(bf16[2048,384]{1,0:T(8,128)(2,1)} %param.14, f32[256,4,384]{0,2,1:T(8,128)} %all-reduce.6.cloned.1.call-done, f32[384]{0:T(512)S(1)} %copy-done.1, f32[4,384]{1,0:T(4,128)S(1)} %concatenate.53), kind=kOutput, calls=%fused_computation.10 | convolution fusion | flops 1611792384 | bytes 11542016 | tf_op jit(solution)/shard_map/rld,vd->rlv/dot_general | solution.py:99
  171.5 8.9 %copy.57 = f32[256,8192]{1,0:T(8,128)} copy(f32[256,8192]{0,1:T(8,128)} %bitcast.64) | data formatting | bytes 16777216
  182.0 1.7 multiply_reduce_fusion
  184.4 9.2 %all-to-all-start = ((f32[16,16,4]{1,2,0:T(4,128)}), f32[16,16,4]{1,2,0:T(4,128)S(1)}, u32[]{:S(2)}, u32[]{:S(2)}) async-start(f32[16,16,4]{1,2,0:T(4,128)} %copy.44), calls=%async_computation | async-start | bytes 65536 | tf_op jit(solution)/shard_map/all_to_all | solution.py:39
  193.7 7.6 %all-to-all-done = f32[16,16,4]{1,2,0:T(4,128)S(1)} async-done(((f32[16,16,4]{1,2,0:T(4,128)}), f32[16,16,4]{1,2,0:T(4,128)S(1)}, u32[]{:S(2)}, u32[]{:S(2)}) %all-to-all-start) | async-done | bytes 4128 | tf_op jit(solution)/shard_map/all_to_all | solution.py:39
  201.3 49.0 %reduce-scatter.4.cloned.1.call-done = f32[16,8192]{1,0:T(8,128)} async-done(((f32[256,8192]{1,0:T(8,128)}), f32[16,8192]{1,0:T(8,128)}) %reduce-scatter.4.cloned.1.call-update) | async-done | bytes 524304
  250.2 3.5 %copy.58 = f32[16,8192]{0,1:T(8,128)} copy(f32[16,8192]{1,0:T(8,128)} %reduce-scatter.4.cloned.1.call-done) | data formatting | bytes 1048576
  253.7 2.8 fusion.21
  256.6 1.0 select_reduce_fusion
  258.2 8.5 %all-reduce.3 = (f32[16,4]{0,1:T(4,128)S(1)}, f32[16,3]{0,1:T(4,128)S(1)}, f32[16,4]{0,1:T(4,128)S(1)}) all-reduce(f32[16,4]{0,1:T(4,128)S(1)} %get-tuple-element.11, f32[16,3]{0,1:T(4,128)S(1)} %fusion.1, f32[16,4]{0,1:T(4,128)S(1)} %get-tuple-element.10), channel_id=1, replica_groups=mesh['seq_0'=8,'seq_1'=2,'vocab_0'=4,'vocab_1'=4] {'vocab_0'}, use_global_device_ids=true, to_apply=%region_12.13 | all-reduce | flops 176 | bytes 1408 | tf_op jit(solution)/shard_map/psum | solution.py:45
  266.8 8.3 %all-reduce.2 = (f32[16,4]{0,1:T(4,128)S(1)}, f32[16,3]{0,1:T(4,128)S(1)}, f32[16,4]{0,1:T(4,128)S(1)}) all-reduce(f32[16,4]{0,1:T(4,128)S(1)} %get-tuple-element.15, f32[16,3]{0,1:T(4,128)S(1)} %get-tuple-element.16, f32[16,4]{0,1:T(4,128)S(1)} %get-tuple-element.17), channel_id=1, replica_groups=mesh['seq_0'=8,'seq_1'=2,'vocab_0'=4,'vocab_1'=4] {'vocab_1'}, use_global_device_ids=true, to_apply=%region_13.14 | all-reduce | flops 176 | bytes 1408 | tf_op jit(solution)/shard_map/psum | solution.py:45
  275.1 21.6 %all-gather.1 = f32[16,16,7]{1,2,0:T(8,128)S(1)} all-gather(f32[1,16,7]{1,2,0:T(8,128)S(1)} %maximum_bitcast_fusion), channel_id=1, replica_groups=mesh['seq_0'=8,'seq_1'=2,'vocab_0'=4,'vocab_1'=4] {'seq_0','seq_1'}, dimensions={0}, use_global_device_ids=true | all-gather | bytes 7616 | tf_op jit(solution)/shard_map/all_gather | solution.py:126
  (60 shorter events, 8.3 us)
Async XLA Ops:
  7.2 3.4 %copy-start = (bf16[3,1024,384]{2,1,0:T(8,128)(2,1)S(1)}, bf16[3,1024,384]{2,1,0:T(8,128)(2,1)}, u32[]{:S(2)}) copy-start(bf16[3,1024,384]{2,1,0:T(8,128)(2,1)} %param.9) | copy-start | bytes 7077892
  7.2 10.1 %copy-start.3 = (s32[1,32]{1,0:T(1,128)S(1)}, s32[1,32]{1,0:T(1,128)}, u32[]{:S(2)}) copy-start(s32[1,32]{1,0:T(1,128)} %param.17) | copy-start | bytes 388
  7.2 45.5 %all-gather.4.cloned.1.call-start = ((), (), s32[]{:S(2)}) async-start(), calls=%async_computation.2 | async-start | bytes 1769472 | tf_op jit(solution)/shard_map/all_gather | solution.py:18
  16.5 147.3 %all-reduce.6.cloned.1.call-start = ((), (), s32[]{:S(2)}) async-start(), calls=%async_computation.3 | async-start | bytes 3145728 | tf_op jit(solution)/shard_map/psum | solution.py:93
  63.1 0.7 copy-start.2
  63.1 100.8 %copy-start.1 = (f32[384]{0:T(512)S(1)}, f32[384]{0:T(512)}, u32[]{:S(2)}) copy-start(f32[384]{0:T(512)} %param.13) | copy-start | bytes 4612
  63.1 187.1 %reduce-scatter.4.cloned.1.call-start = ((), (), s32[]{:S(2)}) async-start(), calls=%async_computation.4 | async-start | bytes 8912896
  184.4 16.8 %all-to-all-start = ((f32[16,16,4]{1,2,0:T(4,128)}), f32[16,16,4]{1,2,0:T(4,128)S(1)}, u32[]{:S(2)}, u32[]{:S(2)}) async-start(f32[16,16,4]{1,2,0:T(4,128)} %copy.44), calls=%async_computation | async-start | bytes 65536 | tf_op jit(solution)/shard_map/all_to_all | solution.py:39
Sparse Core Ops, SparseCore 0:
  16.7 36.0 all-gather.3
  63.2 100.6 all-reduce.5
  180.5 69.6 reduce-scatter.3
where the time goes:
time: 306 us
  waiting for transfers between devices  170 us (56%)
  blocking collectives  61.9 us (20%)
  local copies, waits for them, and re-layouts  27.5 us (9%)
  between operations  14.6 us (5%)
  matrix products  11.3 us (4%)
  other arithmetic  10.7 us (3%)
  starting transfers between devices  9.37 us (3%)
    psum x1, waiting for transfers between devices, body(): summed = lax.psum(partial_value, VOCAB)  100 us
    unnamed x4, waiting for transfers between devices  49 us
    all_gather x1, blocking collectives, body(): every_result = lax.all_gather(results, SEQ, axis=0, tiled=True)  21.6 us
    all_gather x1, blocking collectives, sent_together(): out = lax.all_gather(both, axis, axis=dim, tiled=True)  18.5 us
    psum x2, blocking collectives, over_axes(): value = lax.psum(value, axis)  16.8 us
    unnamed x12, local copies, waits for them, and re-layouts  14.3 us
    all_gather x1, waiting for transfers between devices, gathered_by_axis(): value = lax.all_gather(value, axis, axis=dim, tiled=True)  13.6 us
    all_to_all x1, starting transfers between devices, summed_on_arrival(): lax.all_to_all(blocks, axis, split_axis=0, concat_axis=0, tiled=True)  9.25 us
  transfers between devices with their start and end apart: 4, of which 4 were waited for; matrix products, arithmetic and copies ran while one was open for 2% of the time, Pallas kernels for 0%

commit v1 on v0

--- a/solution.py
+++ b/solution.py
@@ -42,7 +42,7 @@
 
 def over_axes(value, axes):
     for axis in axes:
-        value = lax.psum(value, axis)
+        value = jnp.sum(lax.all_gather(value, axis), axis=0)
     return value
 
 

time: 306 us -> 354 us (1.16)
  blocking collectives: 61.9 us -> 105 us
    all_gather x0 -> x6, blocking collectives: none -> 49.3 us  [over_axes(): value = jnp.sum(lax.all_gather(value, axis), axis=0)]
    psum x2 -> x0, blocking collectives: 16.8 us -> none  [over_axes(): value = lax.psum(value, axis)]
    all_gather x1, blocking collectives: 21.6 us -> 32.5 us  [body(): every_result = lax.all_gather(results, SEQ, axis=0, tiled=True)]
    unnamed x12 -> x16, local copies, waits for them, and re-layouts: 14.3 us -> 15.4 us
where the time goes in v1:
time: 354 us; the launch traced here: 353 us
  waiting for transfers between devices  170 us (48%)
  blocking collectives  105 us (30%)
  local copies, waits for them, and re-layouts  29.5 us (8%)
  between operations  14.6 us (4%)
  other arithmetic  13.6 us (4%)
  matrix products  11.3 us (3%)
  starting transfers between devices  9.37 us (3%)
    psum x1, waiting for transfers between devices, body(): summed = lax.psum(partial_value, VOCAB)  100 us
    all_gather x6, blocking collectives, over_axes(): value = jnp.sum(lax.all_gather(value, axis), axis=0)  49.3 us
    unnamed x4, waiting for transfers between devices  48.3 us
    all_gather x1, blocking collectives, body(): every_result = lax.all_gather(results, SEQ, axis=0, tiled=True)  32.5 us
    all_gather x1, blocking collectives, sent_together(): out = lax.all_gather(both, axis, axis=dim, tiled=True)  18.5 us
    unnamed x16, local copies, waits for them, and re-layouts  15.4 us
    all_gather x1, waiting for transfers between devices, gathered_by_axis(): value = lax.all_gather(value, axis, axis=dim, tiled=True)  13.6 us
    all_to_all x1, starting transfers between devices, summed_on_arrival(): lax.all_to_all(blocks, axis, split_axis=0, concat_axis=0, tiled=True)  9.25 us
  transfers between devices with their start and end apart: 4, of which 4 were waited for; matrix products, arithmetic and copies ran while one was open for 2% of the time, Pallas kernels for 0%

profile of v1, /device:TPU:1, one launch (start us, length us, event | category | flops | bytes accessed | tf_op | source)
XLA Modules:
  0.0 353.1 jit_solution(16213633992920890545)
XLA Ops:
  8.7 1.9 gather_fusion.2
  11.6 4.9 %all_gather.49 = bf16[4,64,384]{2,1,0:T(8,128)(2,1)} all-gather(bf16[4,32,384]{2,1,0:T(8,128)(2,1)S(1)} %pad_maximum_fusion), channel_id=1, replica_groups=mesh['seq_0'=8,'seq_1'=2,'vocab_0'=4,'vocab_1'=4] {'seq_1'}, dimensions={1}, use_global_device_ids=true | all-gather | bytes 294912 | tf_op jit(solution)/shard_map/all_gather | solution.py:18
  17.3 18.5 %all-gather.6 = s32[16,1,33]{2,1,0:T(1,128)S(1)} all-gather(s32[1,1,33]{2,1,0:T(1,128)S(1)} %add_bitcast_fusion), channel_id=1, replica_groups=mesh['seq_0'=8,'seq_1'=2,'vocab_0'=4,'vocab_1'=4] {'seq_0','seq_1'}, dimensions={0}, use_global_device_ids=true | all-gather | bytes 2244 | tf_op jit(solution)/shard_map/all_gather | solution.py:27
  37.1 1.9 gather_fusion
  39.1 13.6 %all-gather.16.cloned.1.call-done = bf16[4,512,384]{2,1,0:T(8,128)(2,1)} async-done(((bf16[4,64,384]{2,1,0:T(8,128)(2,1)}), bf16[4,512,384]{2,1,0:T(8,128)(2,1)}) %all-gather.16.cloned.1.call-update) | async-done | bytes 1572880 | tf_op jit(solution)/shard_map/all_gather | solution.py:18
  52.7 3.8 %copy.39 = bf16[4,512,384]{2,0,1:T(4,128)(2,1)} copy(bf16[4,512,384]{2,1,0:T(8,128)(2,1)} %all-gather.16.cloned.1.call-done) | data formatting | bytes 3145728 | tf_op jit(solution)/shard_map/all_gather | solution.py:18
  56.5 2.9 gather_fusion.3
  59.4 1.9 convolution_bitcast_fusion
  63.8 100.1 %all-reduce.4.cloned.1.call-done = f32[256,4,384]{0,2,1:T(8,128)} async-done(((f32[256,4,384]{0,2,1:T(8,128)}), f32[256,4,384]{0,2,1:T(8,128)}) %all-reduce.4.cloned.1.call-update) | async-done | bytes 1572880 | tf_op jit(solution)/shard_map/psum | solution.py:93
  163.9 7.6 %fusion.2 = f32[256,4,2048]{0,2,1:T(8,128)} fusion(bf16[2048,384]{1,0:T(8,128)(2,1)} %param.14, f32[256,4,384]{0,2,1:T(8,128)} %all-reduce.4.cloned.1.call-done, f32[384]{0:T(512)S(1)} %copy-done.3, f32[4,384]{1,0:T(4,128)S(1)} %concatenate.53), kind=kOutput, calls=%fused_computation.10 | convolution fusion | flops 1611792384 | bytes 11542016 | tf_op jit(solution)/shard_map/rld,vd->rlv/dot_general | solution.py:99
  171.5 8.9 %copy.57 = f32[256,8192]{1,0:T(8,128)} copy(f32[256,8192]{0,1:T(8,128)} %bitcast.70) | data formatting | bytes 16777216
  185.1 9.2 %all-to-all-start = ((f32[16,16,4]{1,2,0:T(4,128)}), f32[16,16,4]{1,2,0:T(4,128)S(1)}, u32[]{:S(2)}, u32[]{:S(2)}) async-start(f32[16,16,4]{1,2,0:T(4,128)} %copy.44), calls=%async_computation | async-start | bytes 65536 | tf_op jit(solution)/shard_map/all_to_all | solution.py:39
  194.4 7.6 %all-to-all-done = f32[16,16,4]{1,2,0:T(4,128)S(1)} async-done(((f32[16,16,4]{1,2,0:T(4,128)}), f32[16,16,4]{1,2,0:T(4,128)S(1)}, u32[]{:S(2)}, u32[]{:S(2)}) %all-to-all-start) | async-done | bytes 4128 | tf_op jit(solution)/shard_map/all_to_all | solution.py:39
  202.0 48.3 %reduce-scatter.4.cloned.1.call-done = f32[16,8192]{1,0:T(8,128)} async-done(((f32[256,8192]{1,0:T(8,128)}), f32[16,8192]{1,0:T(8,128)}) %reduce-scatter.4.cloned.1.call-update) | async-done | bytes 524304
  250.2 3.5 copy.58
  253.7 2.8 fusion.21
  259.8 8.5 %all-gather.9 = f32[4,16,4]{1,2,0:T(4,128)S(1)} all-gather(f32[1,16,4]{1,2,0:T(4,128)S(1)} %bitcast.76), channel_id=4, replica_groups=mesh['seq_0'=8,'seq_1'=2,'vocab_0'=4,'vocab_1'=4] {'vocab_0'}, dimensions={0}, use_global_device_ids=true | all-gather | bytes 1280 | tf_op jit(solution)/shard_map/all_gather | solution.py:45
  268.3 8.3 %all-gather.10 = f32[4,16,4]{1,2,0:T(4,128)S(1)} all-gather(f32[1,16,4]{1,2,0:T(4,128)S(1)} %bitcast.78), channel_id=5, replica_groups=mesh['seq_0'=8,'seq_1'=2,'vocab_0'=4,'vocab_1'=4] {'vocab_1'}, dimensions={0}, use_global_device_ids=true | all-gather | bytes 1280 | tf_op jit(solution)/shard_map/all_gather | solution.py:45
  276.6 8.1 %all-gather.7 = f32[4,16,4]{1,2,0:T(4,128)S(1)} all-gather(f32[1,16,4]{1,2,0:T(4,128)S(1)} %bitcast.75), channel_id=2, replica_groups=mesh['seq_0'=8,'seq_1'=2,'vocab_0'=4,'vocab_1'=4] {'vocab_0'}, dimensions={0}, use_global_device_ids=true | all-gather | bytes 1280 | tf_op jit(solution)/shard_map/all_gather | solution.py:45
  284.7 8.1 %all-gather.8 = f32[4,16,4]{1,2,0:T(4,128)S(1)} all-gather(f32[1,16,4]{1,2,0:T(4,128)S(1)} %bitcast.79), channel_id=3, replica_groups=mesh['seq_0'=8,'seq_1'=2,'vocab_0'=4,'vocab_1'=4] {'vocab_1'}, dimensions={0}, use_global_device_ids=true | all-gather | bytes 1280 | tf_op jit(solution)/shard_map/all_gather | solution.py:45
  292.9 2.6 fusion.1
  295.5 8.1 %all-gather.11 = f32[4,16,3]{1,2,0:T(4,128)S(1)} all-gather(f32[1,16,3]{1,2,0:T(4,128)S(1)} %bitcast.77), channel_id=6, replica_groups=mesh['seq_0'=8,'seq_1'=2,'vocab_0'=4,'vocab_1'=4] {'vocab_0'}, dimensions={0}, use_global_device_ids=true | all-gather | bytes 960 | tf_op jit(solution)/shard_map/all_gather | solution.py:45
  303.7 8.1 %all-gather.12 = f32[4,16,3]{1,2,0:T(4,128)S(1)} all-gather(f32[1,16,3]{1,2,0:T(4,128)S(1)} %bitcast.80), channel_id=7, replica_groups=mesh['seq_0'=8,'seq_1'=2,'vocab_0'=4,'vocab_1'=4] {'vocab_1'}, dimensions={0}, use_global_device_ids=true | all-gather | bytes 960 | tf_op jit(solution)/shard_map/all_gather | solution.py:45
  311.9 32.5 %all-gather.13 = f32[16,16,7]{1,2,0:T(8,128)S(1)} all-gather(f32[1,16,7]{1,2,0:T(8,128)S(1)} %maximum_bitcast_fusion), channel_id=1, replica_groups=mesh['seq_0'=8,'seq_1'=2,'vocab_0'=4,'vocab_1'=4] {'seq_0','seq_1'}, dimensions={0}, use_global_device_ids=true | all-gather | bytes 7616 | tf_op jit(solution)/shard_map/all_gather | solution.py:126
  (74 shorter events, 16.8 us)
Async XLA Ops:
  7.2 3.4 copy-start
  7.2 10.1 %copy-start.5 = (s32[1,32]{1,0:T(1,128)S(1)}, s32[1,32]{1,0:T(1,128)}, u32[]{:S(2)}) copy-start(s32[1,32]{1,0:T(1,128)} %param.17) | copy-start | bytes 388
  7.2 45.5 %all-gather.16.cloned.1.call-start = ((), (), s32[]{:S(2)}) async-start(), calls=%async_computation.2 | async-start | bytes 1769472 | tf_op jit(solution)/shard_map/all_gather | solution.py:18
  16.5 147.3 %all-reduce.4.cloned.1.call-start = ((), (), s32[]{:S(2)}) async-start(), calls=%async_computation.3 | async-start | bytes 3145728 | tf_op jit(solution)/shard_map/psum | solution.py:93
  63.1 0.7 copy-start.4
  63.1 100.8 %copy-start.3 = (f32[384]{0:T(512)S(1)}, f32[384]{0:T(512)}, u32[]{:S(2)}) copy-start(f32[384]{0:T(512)} %param.13) | copy-start | bytes 4612
  63.1 187.1 %reduce-scatter.4.cloned.1.call-start = ((), (), s32[]{:S(2)}) async-start(), calls=%async_computation.4 | async-start | bytes 8912896
  185.1 16.8 %all-to-all-start = ((f32[16,16,4]{1,2,0:T(4,128)}), f32[16,16,4]{1,2,0:T(4,128)S(1)}, u32[]{:S(2)}, u32[]{:S(2)}) async-start(f32[16,16,4]{1,2,0:T(4,128)} %copy.44), calls=%async_computation | async-start | bytes 65536 | tf_op jit(solution)/shard_map/all_to_all | solution.py:39
  256.5 2.2 copy-start.1
  256.6 1.1 copy-start.2
Sparse Core Ops, SparseCore 0:
  16.7 36.0 all-gather.15
  63.2 100.6 all-reduce.3
  180.5 69.6 reduce-scatter.3
